TPU v7x, 32 devices: a whole 2x2x4 slice. The times are simulated.
32 devices in a mesh: dp: 4 (over x, core), param: 8 (over z, y).
Axes of the slice: x: 2, y: 2, z: 4, core: 2. Of those that a mesh axis runs over, the one named last changes fastest.
Arguments:
- train_grads: bfloat16 [3584, 212992], P('dp', 'param'), as said below
- query_grads: bfloat16 [128, 212992], P('dp', 'param'), as said below
Outputs:
- scores: float32 [128, 3584], P('param', 'dp')
Inputs may be any that keep to these rules, and one draw needn't show every extreme that they name: `train_grads`: finite real values. `query_grads`: finite real values.
All inputs are finite; a program needn't handle non-finite values.
Results may differ from a plain program's by a relative error of at most 0.0003.
Values may be sent and summed in bfloat16 or wider, within the bound.
A program may use at most 128 MiB of HBM per device.

v0:
```python
import functools

import jax
import jax.numpy as jnp
from jax import lax
from jax.experimental import pallas as pl
from jax.experimental.pallas import tpu as pltpu
from jax.sharding import PartitionSpec as P

epsilon = 1e-06
lanes = 128
max_chunk = 2048
ahead = 2
block_rows = 256


def chunk_width(width):
    best = lanes
    for tiles in range(1, max_chunk // lanes + 1):
        if width % (tiles * lanes) == 0:
            best = tiles * lanes
    return best


def nt_dot(a, b):
    return lax.dot_general(a, b, (((1,), (1,)), ((), ())), preferred_element_type=jnp.float32)


def kernel(
    cfg, train_hbm, query_hbm, out_ref,
    train, first_q, second_q, first_sum, second_sum, norm_sum, parts, norm_parts,
    train_sem, self_sem, x_send, x_recv, mate_send, mate_recv, fwd_send, fwd_recv,
    part_send, part_recv, norm_send, norm_recv,
):
    chips, params, chunks, width, rows, unit, count, owned, piece = cfg
    dp = lax.axis_index("dp")
    me = lax.axis_index("param")
    chip, core = dp // 2, lax.rem(dp, 2)
    mate = chip * 2 + (1 - core)
    base = 2 * rows
    steps = 2 * chunks

    def columns(c):
        return pl.ds(pl.multiple_of(c * width, width), width)

    def train_copy(c):
        return pltpu.make_async_copy(train_hbm.at[:, columns(c)], train.at[c], train_sem.at[c])

    def self_copy(c):
        return pltpu.make_async_copy(
            query_hbm.at[:, columns(c)], first_q.at[c, pl.ds(0, rows), :], self_sem.at[c]
        )

    def mate_copy(c):
        return pltpu.make_async_remote_copy(
            src_ref=query_hbm.at[:, columns(c)],
            dst_ref=first_q.at[c, pl.ds(rows, rows), :],
            send_sem=mate_send.at[c],
            recv_sem=mate_recv.at[c],
            device_id={"dp": mate},
        )

    def slot(group, c, place):
        if group == 0:
            return first_q.at[c, pl.ds(base + unit * place, unit), :]
        return second_q.at[c, pl.ds(unit * place, unit), :]

    def x_copy(group, c, d):
        start = pl.multiple_of(lax.rem(group + core, 2) * unit, unit)
        return pltpu.make_async_remote_copy(
            src_ref=query_hbm.at[pl.ds(start, unit), columns(c)],
            dst_ref=slot(group, c, 2 * (d - 1)),
            send_sem=x_send.at[d - 1, group * chunks + c],
            recv_sem=x_recv.at[d - 1, group * chunks + c],
            device_id={"dp": lax.rem(chip + d, chips) * 2 + core},
        )

    def fwd_copy(group, c, d):
        return pltpu.make_async_remote_copy(
            src_ref=slot(group, c, 2 * (d - 1)),
            dst_ref=slot(group, c, 2 * (d - 1) + 1),
            send_sem=fwd_send.at[d - 1, group * chunks + c],
            recv_sem=fwd_recv.at[d - 1, group * chunks + c],
            device_id={"dp": mate},
        )

    def pump(group, c):
        for d in range(1, chips):
            x_copy(group, c, d).wait_recv()
            fwd_copy(group, c, d).start()

    def piece_list(group):
        out = []
        if group == 0:
            for source, at in ((dp, 0), (mate, rows)):
                for r in range(0, rows, piece):
                    out.append((first_sum, at + r, source * rows + r))
        for d in range(1, chips):
            other = lax.rem(chip - d + chips, chips)
            for k in range(2):
                from_core = core if k == 0 else 1 - core
                start = lax.rem(group + from_core, 2) * unit
                at = unit * (2 * (d - 1) + k)
                for r in range(0, unit, piece):
                    row = (other * 2 + from_core) * rows + start + r
                    if group == 0:
                        out.append((first_sum, base + at + r, row))
                    else:
                        out.append((second_sum, at + r, row))
        return out

    first_pieces, second_pieces = piece_list(0), piece_list(1)

    def part_copy(index, item):
        buffer, at, row = item
        owner, offset = row // owned, lax.rem(row, owned)
        return owner, offset, pltpu.make_async_remote_copy(
            src_ref=buffer.at[pl.ds(at, piece), :],
            dst_ref=parts.at[me, pl.ds(pl.multiple_of(offset, piece), piece), :],
            send_sem=part_send.at[index],
            recv_sem=part_recv.at[me, offset // piece],
            device_id={"param": owner},
        )

    def send_parts(first_index, items):
        for i, item in enumerate(items):
            owner, offset, copy = part_copy(first_index + i, item)

            @pl.when(owner != me)
            def _():
                copy.start()

            @pl.when(owner == me)
            def _():
                buffer, at, _row = item
                parts[me, pl.ds(pl.multiple_of(offset, piece), piece), :] = buffer[pl.ds(at, piece), :]

    def wait_parts_sent(first_index, items):
        for i, item in enumerate(items):
            owner, _offset, copy = part_copy(first_index + i, item)

            @pl.when(owner != me)
            def _():
                copy.wait_send()

    def norm_copy(j):
        return pltpu.make_async_remote_copy(
            src_ref=norm_parts.at[me],
            dst_ref=norm_parts.at[me],
            send_sem=norm_send.at[j],
            recv_sem=norm_recv.at[me],
            device_id={"param": lax.rem(me + j, params)},
        )

    @pl.loop(0, chunks)
    def _(c):
        train_copy(c).start()
        self_copy(c).start()

    barrier = pltpu.get_barrier_semaphore()
    pl.semaphore_signal(barrier, inc=1, device_id={"dp": mate})
    for d in range(1, chips):
        pl.semaphore_signal(barrier, inc=1, device_id={"dp": lax.rem(chip + d, chips) * 2 + core})
    for j in range(1, params):
        pl.semaphore_signal(barrier, inc=1, device_id={"param": lax.rem(me + j, params)})
    pl.semaphore_wait(barrier, chips + params - 1)

    @pl.loop(0, chunks)
    def _(c):
        for d in range(1, chips):
            x_copy(0, c, d).start()
        mate_copy(c).start()

    @pl.loop(0, chunks)
    def _(c):
        for d in range(1, chips):
            x_copy(1, c, d).start()

    first_sum[...] = jnp.zeros_like(first_sum)
    second_sum[...] = jnp.zeros_like(second_sum)
    norm_sum[...] = jnp.zeros_like(norm_sum)

    def add_query_norm(total, q):
        acc = total[:, pl.ds(count, lanes)]
        for k in range(0, width, lanes):
            x = q[:, k : k + lanes].astype(jnp.float32)
            acc = acc + x * x
        total[:, pl.ds(count, lanes)] = acc

    for c in range(ahead):
        pump(0, c)

    @pl.loop(0, chunks)
    def _(c):
        @pl.when(c + ahead < chunks)
        def _():
            pump(0, c + ahead)

        @pl.when(c + ahead >= chunks)
        def _():
            pump(1, c + ahead - chunks)

        train_copy(c).wait()
        self_copy(c).wait()
        mate_copy(c).wait_recv()
        for d in range(1, chips):
            fwd_copy(0, c, d).wait_recv()
        q = first_q[c]
        add_query_norm(first_sum, q)
        for r in range(0, count, block_rows):
            size = min(block_rows, count - r)
            t = train[c, pl.ds(r, size), :]
            first_sum[:, pl.ds(r, size)] += nt_dot(q, t)
            for s in range(0, size, lanes):
                acc = norm_sum[pl.ds(r + s, lanes), :]
                for k in range(0, width, lanes):
                    x = t[s : s + lanes, k : k + lanes].astype(jnp.float32)
                    acc = acc + x * x
                norm_sum[pl.ds(r + s, lanes), :] = acc

    totals = [
        jnp.sum(norm_sum[pl.ds(r, lanes), :].T, axis=0, keepdims=True) for r in range(0, count, lanes)
    ]
    spare = norm_parts.shape[1] - len(totals)
    if spare:
        totals.append(jnp.zeros((spare, lanes), jnp.float32))
    norm_parts[me] = jnp.concatenate(totals, axis=0)
    send_parts(0, first_pieces)
    for j in range(1, params):
        norm_copy(j).start()

    @pl.loop(0, chunks)
    def _(c):
        @pl.when(c + ahead < chunks)
        def _():
            pump(1, c + ahead)

        for d in range(1, chips):
            fwd_copy(1, c, d).wait_recv()
        q = second_q[c]
        add_query_norm(second_sum, q)
        for r in range(0, count, block_rows):
            size = min(block_rows, count - r)
            second_sum[:, pl.ds(r, size)] += nt_dot(q, train[c, pl.ds(r, size), :])

    send_parts(len(first_pieces), second_pieces)

    @pl.loop(0, chunks)
    def _(c):
        mate_copy(c).wait_send()
        for d in range(1, chips):
            for group in range(2):
                x_copy(group, c, d).wait_send()
                fwd_copy(group, c, d).wait_send()

    norm = norm_parts[me]
    for j in range(1, params):
        other = lax.rem(me + j, params)
        pltpu.make_async_copy(norm_parts.at[other], norm_parts.at[other], norm_recv.at[other]).wait()
        norm = norm + norm_parts[other]
        norm_copy(j).wait_send()
    train_scale = lax.rsqrt(norm + epsilon)

    total = parts[me]
    for j in range(1, params):
        other = lax.rem(me + j, params)
        for k in range(owned // piece):
            place = parts.at[other, pl.ds(k * piece, piece), :]
            pltpu.make_async_copy(place, place, part_recv.at[other, k]).wait()
        total = total + parts[other]
    query_norm = jnp.sum(total[:, count:], axis=1, keepdims=True)
    query_scale = lax.rsqrt(query_norm + epsilon)
    for k in range(count // lanes):
        at = slice(k * lanes, (k + 1) * lanes)
        out_ref[:, at] = total[:, at] * query_scale * train_scale[k : k + 1, :]

    wait_parts_sent(0, first_pieces)
    wait_parts_sent(len(first_pieces), second_pieces)


def solution(mesh):
    chips, params = mesh.shape["dp"] // 2, mesh.shape["param"]

    def per_device(train_grads, query_grads):
        count, total = train_grads.shape
        rows = query_grads.shape[0]
        width = chunk_width(total)
        chunks = total // width
        unit = rows // 2
        owned = rows * chips * 2 // params
        piece = min(unit, owned)
        far = 2 * (chips - 1) * unit
        pieces = (2 * rows + 2 * far) // piece
        cfg = (chips, params, chunks, width, rows, unit, count, owned, piece)
        dma = pltpu.SemaphoreType.DMA
        return pl.pallas_call(
            functools.partial(kernel, cfg),
            out_shape=jax.ShapeDtypeStruct((owned, count), jnp.float32),
            in_specs=[pl.BlockSpec(memory_space=pl.ANY)] * 2,
            out_specs=pl.BlockSpec(memory_space=pltpu.VMEM),
            scratch_shapes=[
                pltpu.VMEM((chunks, count, width), jnp.bfloat16),
                pltpu.VMEM((chunks, 2 * rows + far, width), jnp.bfloat16),
                pltpu.VMEM((chunks, far, width), jnp.bfloat16),
                pltpu.VMEM((2 * rows + far, count + lanes), jnp.float32),
                pltpu.VMEM((far, count + lanes), jnp.float32),
                pltpu.VMEM((count, lanes), jnp.float32),
                pltpu.VMEM((params, owned, count + lanes), jnp.float32),
                pltpu.VMEM((params, -(-count // lanes // 8) * 8, lanes), jnp.float32),
                dma((chunks,)),
                dma((chunks,)),
                dma((chips - 1, 2 * chunks)),
                dma((chips - 1, 2 * chunks)),
                dma((chunks,)),
                dma((chunks,)),
                dma((chips - 1, 2 * chunks)),
                dma((chips - 1, 2 * chunks)),
                dma((pieces,)),
                dma((params, owned // piece)),
                dma((params,)),
                dma((params,)),
            ],
            compiler_params=pltpu.CompilerParams(
                collective_id=0, has_side_effects=True, vmem_limit_bytes=62 * 1024 * 1024
            ),
        )(train_grads, query_grads)

    return jax.shard_map(
        per_device,
        mesh=mesh,
        in_specs=(P("dp", "param"), P("dp", "param")),
        out_specs=P("param", "dp"),
        check_vma=False,
    )
```

profile of v0, /device:TPU:6, one launch (start us, length us, event | category | flops | bytes accessed | tf_op | source)
XLA Modules:
  0.0 56.3 jit_solution(8115621115052765514)
XLA Ops:
  0.0 54.8 %shard_map.28 = f32[16,896]{1,0:T(8,128)} custom-call(bf16[896,26624]{1,0:T(8,128)(2,1)} %train_hbm.1, bf16[32,26624]{1,0:T(8,128)(2,1)} %query_hbm.1), custom_call_target="tpu_custom_call" | custom-call | tf_op jit(solution)/shard_map/pallas_call | solution.py:296
  54.8 1.4 %copy.4 = f32[16,896]{1,0:T(8,128)} copy(f32[16,896]{1,0:T(8,128)} %shard_map.28) | data formatting | bytes 114688
where the time goes:
time: 56.4 us; the launch traced here: 56.3 us
  Pallas kernels  54.8 us (97%)
  local copies, waits for them, and re-layouts  1.45 us (3%)
    pallas_call x1, Pallas kernels, per_device(): pl.pallas_call(functools.partial(kernel, cfg), out_shape=jax.ShapeDtypeSt...  54.8 us
    unnamed x1, local copies, waits for them, and re-layouts  1.45 us

commit v1 on v0

v1 whole, which is shorter than its diff:
```python
import functools

import jax
import jax.numpy as jnp
from jax import lax
from jax.experimental import pallas as pl
from jax.experimental.pallas import tpu as pltpu
from jax.sharding import PartitionSpec as P

epsilon = 1e-06
lanes = 128
sublanes = 8
max_chunk = 2048
block_rows = 256
train_width = 1024
x_width = 1024


def chunk_width(width):
    best = lanes
    for tiles in range(1, max_chunk // lanes + 1):
        if width % (tiles * lanes) == 0:
            best = tiles * lanes
    return best


def column_plan(total):
    base = chunk_width(total)
    chunks = total // base
    pairs = (chunks - 1) // 2
    first = [(2 * base * g, 2 * base) for g in range(pairs)]
    first.append((2 * base * pairs, total - 2 * base * pairs))
    looped = max(pairs - 1, 0)
    second = [(2 * base * g, 2 * base) for g in range(looped)]
    at = 2 * base * looped
    fine = 1024 if base % 1024 == 0 else base
    while total - at > 4 * fine:
        size = min(base, total - at - 4 * fine)
        second.append((at, size))
        at += size
    while at < total:
        size = min(fine, total - at)
        second.append((at, size))
        at += size
    return base, pairs, looped, first, second


def nt_dot(a, b):
    return lax.dot_general(a, b, (((1,), (1,)), ((), ())), preferred_element_type=jnp.float32)


def kernel(
    cfg, train_hbm, query_hbm, out_ref,
    train, first_q, second_q, first_sum, second_sum, norm_sum, parts, norm_parts, query_sum, query_scales, scale,
    train_sem, self_sem, x_send, first_recv, second_recv, mate_send, mate_recv,
    fwd_send, first_fwd, second_fwd, part_send, part_recv, norm_send, norm_recv,
    query_send, query_recv, known,
):
    chips, params, total, rows, unit, count, owned, piece, plan = cfg
    base, pairs, looped, first_plan, second_plan = plan
    dp = lax.axis_index("dp")
    me = lax.axis_index("param")
    chip, core = dp // 2, lax.rem(dp, 2)
    mate = chip * 2 + (1 - core)
    cores = 2 * chips
    near = 2 * rows
    x_recv = (first_recv, second_recv)
    fwd_recv = (first_fwd, second_fwd)

    def bytes_wait(ref, sem):
        pltpu.make_async_copy(ref, ref, sem).wait()

    def columns(group, i):
        plan_of = first_plan if group == 0 else second_plan
        if isinstance(i, int):
            start, size = plan_of[i]
            return pl.ds(start, size)
        return pl.ds(pl.multiple_of(i * 2 * base, 2 * base), 2 * base)

    def split(start, size, width):
        return [pl.ds(start + k, min(width, size - k)) for k in range(0, size, width)]

    def train_copies(i):
        return [
            pltpu.make_async_copy(train_hbm.at[:, cols], train.at[:, cols], train_sem.at[i])
            for cols in split(*first_plan[i], train_width)
        ]

    def self_copies(i):
        return [
            pltpu.make_async_copy(query_hbm.at[:, cols], first_q.at[pl.ds(0, rows), cols], self_sem.at[i])
            for cols in split(*first_plan[i], base)
        ]

    def wait_train(i):
        bytes_wait(query_hbm.at[:, columns(0, i)], self_sem.at[i])
        bytes_wait(train.at[:, columns(0, i)], train_sem.at[i])

    def mate_copies(i):
        return [
            pltpu.make_async_remote_copy(
                src_ref=query_hbm.at[:, cols],
                dst_ref=first_q.at[pl.ds(rows, rows), cols],
                send_sem=mate_send.at[0],
                recv_sem=mate_recv.at[0],
                device_id={"dp": mate},
            )
            for cols in split(*first_plan[i], base)
        ]

    def slot(group, i, place):
        if group == 0:
            return first_q.at[pl.ds(near + unit * place, unit), columns(0, i)]
        return second_q.at[pl.ds(unit * place, unit), columns(1, i)]

    def x_copies(group, i, d):
        start = pl.multiple_of(lax.rem(group + core, 2) * unit, unit)
        place = pl.ds((near if group == 0 else 0) + unit * 2 * (d - 1), unit)
        dst = first_q if group == 0 else second_q
        return [
            pltpu.make_async_remote_copy(
                src_ref=query_hbm.at[pl.ds(start, unit), cols],
                dst_ref=dst.at[place, cols],
                send_sem=x_send.at[d - 1],
                recv_sem=x_recv[group].at[d - 1, i],
                device_id={"dp": lax.rem(chip + d, chips) * 2 + core},
            )
            for cols in split(*(first_plan if group == 0 else second_plan)[i], x_width)
        ]

    def fwd_copy(group, i, d):
        return pltpu.make_async_remote_copy(
            src_ref=slot(group, i, 2 * (d - 1)),
            dst_ref=slot(group, i, 2 * (d - 1) + 1),
            send_sem=fwd_send.at[0],
            recv_sem=fwd_recv[group].at[d - 1, i],
            device_id={"dp": mate},
        )

    def pump(group, i):
        for d in range(1, chips):
            bytes_wait(slot(group, i, 2 * (d - 1)), x_recv[group].at[d - 1, i])
            fwd_copy(group, i, d).start()

    def arrive(group, i):
        for d in range(1, chips):
            fwd_copy(group, i, d).wait_recv()

    def piece_list(group):
        out = []
        if group == 0:
            for source, at in ((dp, 0), (mate, rows)):
                for r in range(0, rows, piece):
                    out.append((first_sum, at + r, source * rows + r))
        for d in range(1, chips):
            other = lax.rem(chip - d + chips, chips)
            for k in range(2):
                from_core = core if k == 0 else 1 - core
                start = lax.rem(group + from_core, 2) * unit
                at = unit * (2 * (d - 1) + k)
                for r in range(0, unit, piece):
                    row = (other * 2 + from_core) * rows + start + r
                    if group == 0:
                        out.append((first_sum, near + at + r, row))
                    else:
                        out.append((second_sum, at + r, row))
        return out

    def send_parts(items):
        for buffer, at, row in items:
            owner, offset = row // owned, lax.rem(row, owned)
            place = parts.at[me, pl.ds(pl.multiple_of(offset, piece), piece), :]
            copy = pltpu.make_async_remote_copy(
                src_ref=buffer.at[pl.ds(at, piece), :],
                dst_ref=place,
                send_sem=part_send.at[0],
                recv_sem=part_recv.at[0],
                device_id={"param": owner},
            )

            @pl.when(owner != me)
            def _():
                copy.start()

            @pl.when(owner == me)
            def _():
                place[...] = buffer[pl.ds(at, piece), :]

    def norm_copy(j):
        return pltpu.make_async_remote_copy(
            src_ref=norm_parts.at[me],
            dst_ref=norm_parts.at[me],
            send_sem=norm_send.at[0],
            recv_sem=norm_recv.at[0],
            device_id={"param": lax.rem(me + j, params)},
        )

    def query_copy(j):
        return pltpu.make_async_remote_copy(
            src_ref=query_scales,
            dst_ref=query_scales,
            send_sem=query_send.at[0],
            recv_sem=query_recv.at[0],
            device_id={"dp": lax.rem(dp + j, cores)},
        )

    pairmate = me + 1 - 2 * lax.rem(me, 2)
    neighbours = (pairmate, lax.rem(me + 2, params), lax.rem(me + params - 2, params))
    stages = known.shape[0]

    for i in range(len(first_plan)):
        for copy in self_copies(i) + train_copies(i):
            copy.start()

    barrier = pltpu.get_barrier_semaphore()
    for j in range(1, cores):
        pl.semaphore_signal(barrier, inc=1, device_id={"dp": lax.rem(dp + j, cores)})
    for other in neighbours:
        pl.semaphore_signal(barrier, inc=1, device_id={"param": other})
    pl.semaphore_wait(barrier, cores - 1 + len(neighbours))

    for other in neighbours:
        pl.semaphore_signal(known.at[0], inc=1, device_id={"param": other})
    for i in range(len(first_plan)):
        for d in range(1, chips):
            for copy in x_copies(0, i, d):
                copy.start()
        for copy in mate_copies(i):
            copy.start()
    for i in range(len(second_plan)):
        for d in range(1, chips):
            for copy in x_copies(1, i, d):
                copy.start()

    first_sum[...] = jnp.zeros_like(first_sum)
    second_sum[...] = jnp.zeros_like(second_sum)
    norm_sum[...] = jnp.zeros_like(norm_sum)

    query_sum[...] = jnp.zeros_like(query_sum)

    def next_round(stage):
        pl.semaphore_wait(known.at[stage], len(neighbours))
        if stage + 1 < stages:
            for other in neighbours:
                pl.semaphore_signal(known.at[stage + 1], inc=1, device_id={"param": other})

    def multiply(sums, q_ref, start, width, norms):
        if not isinstance(start, int):
            start = pl.multiple_of(start, base)
        q = q_ref[:, pl.ds(start, width)]
        if norms:
            acc = query_sum[...]
            for k in range(0, width, lanes):
                x = q[:rows, k : k + lanes].astype(jnp.float32)
                acc = acc + x * x
            query_sum[...] = acc
        for r in range(0, count, block_rows):
            size = min(block_rows, count - r)
            t = train[pl.ds(r, size), pl.ds(start, width)]
            sums[:, pl.ds(r, size)] += nt_dot(q, t)
            if norms:
                for s in range(0, size, lanes):
                    acc = norm_sum[pl.ds(r + s, lanes), :]
                    for k in range(0, width, lanes):
                        x = t[s : s + lanes, k : k + lanes].astype(jnp.float32)
                        acc = acc + x * x
                    norm_sum[pl.ds(r + s, lanes), :] = acc

    bytes_wait(query_hbm, mate_recv.at[0])
    pump(0, 0)

    @pl.loop(0, pairs)
    def _(g):
        wait_train(g)
        arrive(0, g)
        multiply(first_sum, first_q, g * 2 * base, base, True)

        @pl.when(g + 1 < pairs)
        def _():
            pump(0, g + 1)

        @pl.when(g + 1 == pairs)
        def _():
            pump(0, pairs)

        multiply(first_sum, first_q, g * 2 * base + base, base, True)

        @pl.when(g == 0)
        def _():
            next_round(0)

    start, size = first_plan[pairs]
    wait_train(pairs)
    arrive(0, pairs)
    for at in range(start, start + size, base):
        multiply(first_sum, first_q, at, base, True)

    for stage in range(1, stages):
        next_round(stage)
    send_parts(piece_list(0))

    totals = [
        jnp.sum(norm_sum[pl.ds(r, lanes), :].T, axis=0, keepdims=True) for r in range(0, count, lanes)
    ]
    query_row = len(totals)
    square = jnp.concatenate([query_sum[...], jnp.zeros((lanes - rows, lanes), jnp.float32)], axis=0)
    totals.append(jnp.sum(square.T, axis=0, keepdims=True))
    spare = norm_parts.shape[1] - len(totals)
    if spare:
        totals.append(jnp.zeros((spare, lanes), jnp.float32))
    norm_parts[me] = jnp.concatenate(totals, axis=0)
    for j in range(1, params):
        norm_copy(j).start()

    first_row = me * owned
    source = first_row // rows

    def share_scales():
        bytes_wait(norm_parts.at[pl.ds(0, params - 1)], norm_send.at[0])
        bytes_wait(norm_parts.at[pl.ds(0, params - 1)], norm_recv.at[0])
        norm = norm_parts[0]
        for j in range(1, params):
            norm = norm + norm_parts[j]
        scale[...] = lax.rsqrt(norm + epsilon)

        @pl.when(dp == source)
        def _():
            query_scales[...] = jnp.broadcast_to(scale[query_row : query_row + 1, :], query_scales.shape)
            for j in range(1, cores):
                query_copy(j).start()

    pump(1, 0)
    if looped:
        @pl.loop(0, looped)
        def _(g):
            arrive(1, g)
            multiply(second_sum, second_q, g * 2 * base, base, False)

            @pl.when(g + 1 < looped)
            def _():
                pump(1, g + 1)

            @pl.when(g + 1 == looped)
            def _():
                pump(1, looped)

            multiply(second_sum, second_q, g * 2 * base + base, base, False)

            @pl.when(g == looped - 1)
            def _():
                share_scales()

    else:
        share_scales()

    last = len(second_plan) - 1
    for i in range(looped, last + 1):
        if i < last:
            pump(1, i + 1)
        arrive(1, i)
        multiply(second_sum, second_q, *second_plan[i], False)

    send_parts(piece_list(1))

    @pl.when(dp == source)
    def _():
        bytes_wait(norm_parts.at[pl.ds(0, cores - 1)], query_send.at[0])

    @pl.when(dp != source)
    def _():
        bytes_wait(query_scales, query_recv.at[0])

    pick = lax.broadcasted_iota(jnp.int32, (owned, lanes), 1) == (
        lax.broadcasted_iota(jnp.int32, (owned, lanes), 0) + lax.rem(first_row, rows)
    )
    query_scale = jnp.sum(jnp.where(pick, query_scales[0:1, :], 0.0), axis=1, keepdims=True)

    bytes_wait(query_hbm, mate_send.at[0])
    for d in range(1, chips):
        bytes_wait(query_hbm, x_send.at[d - 1])
    bytes_wait(second_q, fwd_send.at[0])

    bytes_wait(parts.at[pl.ds(0, params - 1)], part_recv.at[0])
    for k in range(count // lanes):
        at = slice(k * lanes, (k + 1) * lanes)
        products = parts[0, :, at]
        for j in range(1, params):
            products = products + parts[j, :, at]
        out_ref[:, at] = products * query_scale * scale[k : k + 1, :]

    bytes_wait(parts.at[pl.ds(0, params - 1)], part_send.at[0])


def solution(mesh):
    chips, params = mesh.shape["dp"] // 2, mesh.shape["param"]

    def per_device(train_grads, query_grads):
        count, total = train_grads.shape
        rows = query_grads.shape[0]
        unit = rows // 2
        cores = 2 * chips
        owned = rows * cores // params
        piece = min(unit, owned)
        far = 2 * (chips - 1) * unit
        plan = column_plan(total)
        _base, _pairs, _looped, first_plan, second_plan = plan
        cfg = (chips, params, total, rows, unit, count, owned, piece, plan)
        pad = lambda n: -(-n // sublanes) * sublanes
        norm_rows = pad(count // lanes + 1)
        dma = pltpu.SemaphoreType.DMA
        return pl.pallas_call(
            functools.partial(kernel, cfg),
            out_shape=jax.ShapeDtypeStruct((owned, count), jnp.float32),
            in_specs=[pl.BlockSpec(memory_space=pl.ANY)] * 2,
            out_specs=pl.BlockSpec(memory_space=pltpu.VMEM),
            scratch_shapes=[
                pltpu.VMEM((count, total), jnp.bfloat16),
                pltpu.VMEM((2 * rows + far, total), jnp.bfloat16),
                pltpu.VMEM((far, total), jnp.bfloat16),
                pltpu.VMEM((2 * rows + far, count), jnp.float32),
                pltpu.VMEM((far, count), jnp.float32),
                pltpu.VMEM((count, lanes), jnp.float32),
                pltpu.VMEM((params, owned, count), jnp.float32),
                pltpu.VMEM((params, norm_rows, lanes), jnp.float32),
                pltpu.VMEM((rows, lanes), jnp.float32),
                pltpu.VMEM((norm_rows, lanes), jnp.float32),
                pltpu.VMEM((norm_rows, lanes), jnp.float32),
                dma((len(first_plan),)),
                dma((len(first_plan),)),
                dma((chips - 1,)),
                dma((chips - 1, len(first_plan))),
                dma((chips - 1, len(second_plan))),
                dma((1,)),
                dma((1,)),
                dma((1,)),
                dma((chips - 1, len(first_plan))),
                dma((chips - 1, len(second_plan))),
                dma((1,)),
                dma((1,)),
                dma((1,)),
                dma((1,)),
                dma((1,)),
                dma((1,)),
                pltpu.SemaphoreType.REGULAR((params // 4,)),
            ],
            compiler_params=pltpu.CompilerParams(
                collective_id=0, has_side_effects=True, vmem_limit_bytes=62 * 1024 * 1024
            ),
        )(train_grads, query_grads)

    return jax.shard_map(
        per_device,
        mesh=mesh,
        in_specs=(P("dp", "param"), P("dp", "param")),
        out_specs=P("param", "dp"),
        check_vma=False,
    )
```

time: 56.4 us -> 55.6 us (0.986); the launches traced: 56.3 us -> 54.9 us
  Pallas kernels: 54.8 us -> 53.4 us
    pallas_call x1, Pallas kernels: 54.8 us -> 53.4 us  [per_device(): pl.pallas_call(functools.partial(kernel, cfg), out_shape=jax.ShapeDtypeSt...]
where the time goes in v1:
time: 55.6 us; the launch traced here: 54.9 us
  Pallas kernels  53.4 us (96%)
  local copies, waits for them, and re-layouts  1.45 us (3%)
    pallas_call x1, Pallas kernels, per_device(): pl.pallas_call(functools.partial(kernel, cfg), out_shape=jax.ShapeDtypeSt...  53.4 us
    unnamed x1, local copies, waits for them, and re-layouts  1.45 us

profile of v1, /device:TPU:6, one launch (start us, length us, event | category | flops | bytes accessed | tf_op | source)
XLA Modules:
  0.0 54.9 jit_solution(2038366735623470363)
XLA Ops:
  0.0 53.4 %shard_map.28 = f32[16,896]{1,0:T(8,128)} custom-call(bf16[896,26624]{1,0:T(8,128)(2,1)} %train_hbm.1, bf16[32,26624]{1,0:T(8,128)(2,1)} %query_hbm.1), custom_call_target="tpu_custom_call" | custom-call | tf_op jit(solution)/shard_map/pallas_call | solution.py:411
  53.4 1.4 %copy.4 = f32[16,896]{1,0:T(8,128)} copy(f32[16,896]{1,0:T(8,128)} %shard_map.28) | data formatting | bytes 114688

commit v2 on v1

--- a/solution.py
+++ b/solution.py
@@ -30,18 +30,10 @@
     pairs = (chunks - 1) // 2
     first = [(2 * base * g, 2 * base) for g in range(pairs)]
     first.append((2 * base * pairs, total - 2 * base * pairs))
-    looped = max(pairs - 1, 0)
-    second = [(2 * base * g, 2 * base) for g in range(looped)]
-    at = 2 * base * looped
+    looped = max(chunks - 2, 0)
+    second = [(base * c, base) for c in range(looped)]
     fine = 1024 if base % 1024 == 0 else base
-    while total - at > 4 * fine:
-        size = min(base, total - at - 4 * fine)
-        second.append((at, size))
-        at += size
-    while at < total:
-        size = min(fine, total - at)
-        second.append((at, size))
-        at += size
+    second += [(at, fine) for at in range(base * looped, total, fine)]
     return base, pairs, looped, first, second
 
 
@@ -75,7 +67,8 @@
         if isinstance(i, int):
             start, size = plan_of[i]
             return pl.ds(start, size)
-        return pl.ds(pl.multiple_of(i * 2 * base, 2 * base), 2 * base)
+        width = 2 * base if group == 0 else base
+        return pl.ds(pl.multiple_of(i * width, width), width)
 
     def split(start, size, width):
         return [pl.ds(start + k, min(width, size - k)) for k in range(0, size, width)]
@@ -332,21 +325,19 @@
     pump(1, 0)
     if looped:
         @pl.loop(0, looped)
-        def _(g):
-            arrive(1, g)
-            multiply(second_sum, second_q, g * 2 * base, base, False)
-
-            @pl.when(g + 1 < looped)
+        def _(c):
+            @pl.when(c + 1 < looped)
             def _():
-                pump(1, g + 1)
-
-            @pl.when(g + 1 == looped)
+                pump(1, c + 1)
+
+            @pl.when(c + 1 == looped)
             def _():
                 pump(1, looped)
 
-            multiply(second_sum, second_q, g * 2 * base + base, base, False)
-
-            @pl.when(g == looped - 1)
+            arrive(1, c)
+            multiply(second_sum, second_q, c * base, base, False)
+
+            @pl.when(c == max(looped - 3, 0))
             def _():
                 share_scales()
 
@@ -354,9 +345,11 @@
         share_scales()
 
     last = len(second_plan) - 1
+    if looped < last:
+        pump(1, looped + 1)
     for i in range(looped, last + 1):
-        if i < last:
-            pump(1, i + 1)
+        if i + 2 <= last:
+            pump(1, i + 2)
         arrive(1, i)
         multiply(second_sum, second_q, *second_plan[i], False)
 

time: 55.6 us -> 55.3 us (level)
  Pallas kernels: 53.4 us -> 52.8 us
    pallas_call x1, Pallas kernels: 53.4 us -> 52.8 us  [per_device(): pl.pallas_call(functools.partial(kernel, cfg), out_shape=jax.ShapeDtypeSt...]
where the time goes in v2:
time: 55.3 us; the launch traced here: 54.2 us
  Pallas kernels  52.8 us (95%)
  local copies, waits for them, and re-layouts  1.45 us (3%)
    pallas_call x1, Pallas kernels, per_device(): pl.pallas_call(functools.partial(kernel, cfg), out_shape=jax.ShapeDtypeSt...  52.8 us
    unnamed x1, local copies, waits for them, and re-layouts  1.45 us

profile of v2, /device:TPU:6, one launch (start us, length us, event | category | flops | bytes accessed | tf_op | source)
XLA Modules:
  0.0 54.2 jit_solution(7517060553763848446)
XLA Ops:
  0.0 52.8 %shard_map.28 = f32[16,896]{1,0:T(8,128)} custom-call(bf16[896,26624]{1,0:T(8,128)(2,1)} %train_hbm.1, bf16[32,26624]{1,0:T(8,128)(2,1)} %query_hbm.1), custom_call_target="tpu_custom_call" | custom-call | tf_op jit(solution)/shard_map/pallas_call | solution.py:404
  52.8 1.4 %copy.4 = f32[16,896]{1,0:T(8,128)} copy(f32[16,896]{1,0:T(8,128)} %shard_map.28) | data formatting | bytes 114688
